TPU v7x, 32 devices: a whole 2x2x4 slice. The times are simulated.
32 devices in a mesh: blk: 8 (over z, y), sub: 4 (over x, core).
Axes of the slice: x: 2, y: 2, z: 4, core: 2. Of those that a mesh axis runs over, the one named last changes fastest.
Arguments:
- integrals: float32 [32, 4, 32, 6144], P('blk', 'sub'), may hold values from -1 to 1
- slot_order: int32 [32, 4, 32], P('blk', 'sub'), may hold values from 0 to 31, each once within a row
- factor_rows: float32 [32, 4, 32, 4096], P(None, 'sub'), may hold values from -1 to 1.5, as said below
- occ_energy: float32 [384], replicated, may hold values from -1.5 to -0.3
- slab_index: int32 [1], replicated, may hold values from 0 to 127
- virt_energy: float32 [2048], replicated, may hold values from 0.1 to 3
Outputs:
- amplitudes: float32 [6144, 6144], P('blk', 'sub')
Inputs may be any that keep to these rules, and one draw needn't show every extreme that they name: `slot_order`: each row of 32 entries holds every number from 0 to 31 once. `factor_rows`: the factor is lower triangular (zero above its diagonal) with diagonal entries between 0.5 and 1.5.
All inputs are finite; a program needn't handle non-finite values.
Results may differ from a plain program's by a relative error of at most 0.0001.
Values sent between devices are 32-bit elements; how exact they have to be, the bound alone decides.
A program may use at most 128 MiB of HBM per device.

v0:
```python
import jax
import jax.numpy as jnp
from jax import lax
from jax.sharding import PartitionSpec as P

NVIRT = 2048
NOCC = 3
PRECISE = lax.Precision.HIGHEST


def canonical_order(integrals, slot_order):
    piece_len = integrals.shape[2]
    places = jnp.arange(piece_len, dtype=jnp.int32)
    onehot = (slot_order[..., None] == places).astype(jnp.float32)
    return jnp.einsum("rscq,rscp->rsqp", onehot, integrals, precision=PRECISE)


def transposed_dot(left, right):
    return lax.dot_general(left, right, (((0,), (0,)), ((), ())), precision=PRECISE)


def after_section(solved, own_rows, rhs_rows, diag_inverse, first, reach):
    round_width = diag_inverse.shape[1]
    pair_cols = solved.shape[2]
    width = reach * round_width
    rows_part = own_rows[:, :, :width]

    def advance(round_id, solved):
        factor_part = lax.dynamic_index_in_dim(rows_part, round_id, 0, keepdims=False)
        known_part = jnp.dot(
            factor_part, solved[:reach].reshape(width, pair_cols), precision=PRECISE
        )
        updated = lax.dynamic_index_in_dim(rhs_rows, round_id, 0, keepdims=False) - known_part
        round_block = lax.all_gather(updated[None], "sub", axis=0, tiled=True).reshape(
            round_width, pair_cols
        )
        inverse = lax.dynamic_index_in_dim(diag_inverse, round_id, 0, keepdims=False)
        solved_round = jnp.dot(inverse, round_block, precision=PRECISE)
        return lax.dynamic_update_index_in_dim(solved, solved_round, round_id, 0)

    return lax.fori_loop(first, reach, advance, solved, unroll=True)


def shards(integrals, slot_order, factor_rows, occ_energy, slab_index, virt_energy):
    canonical = canonical_order(integrals, slot_order)
    local_rhs = lax.all_to_all(canonical, "blk", split_axis=3, concat_axis=0, tiled=True)
    rounds = factor_rows.shape[0]
    piece_len = factor_rows.shape[2]
    sub_count = lax.axis_size("sub")
    round_width = sub_count * piece_len
    pair_cols = local_rhs.shape[3]
    shaped = factor_rows.reshape(rounds, piece_len, rounds, round_width)
    round_ids = jnp.arange(rounds)
    own_diag = shaped[round_ids, :, round_ids, :]
    diag_blocks = lax.all_gather(own_diag[:, None], "sub", axis=1, tiled=True).reshape(
        rounds, round_width, round_width
    )
    identity = jnp.broadcast_to(
        jnp.eye(round_width, dtype=jnp.float32), (rounds, round_width, round_width)
    )
    diag_inverse = jax.scipy.linalg.solve_triangular(diag_blocks, identity, lower=True)
    rhs_rows = local_rhs[:, 0]
    own_rows = factor_rows[:, 0]
    solved_start = jnp.zeros((rounds, round_width, pair_cols), jnp.float32)
    section_count = min(8, rounds)
    per_section = rounds // section_count
    solved = solved_start
    for section_id in range(section_count):
        solved = after_section(
            solved,
            own_rows,
            rhs_rows,
            diag_inverse,
            section_id * per_section,
            (section_id + 1) * per_section,
        )
    sub_index = lax.axis_index("sub")
    total_pairs = pair_cols * lax.axis_size("blk")
    quarter = total_pairs // sub_count
    solved_full = solved.reshape(rounds, sub_count, piece_len, pair_cols)
    own_part = lax.dynamic_index_in_dim(solved_full, sub_index, 1, keepdims=False).reshape(
        rounds * piece_len, pair_cols
    )
    product = transposed_dot(own_part, lax.all_gather(own_part, "blk", axis=1, tiled=True))
    coulomb = lax.psum_scatter(product, "sub", scatter_dimension=1, tiled=True)
    slab_start = slab_index[0] * NOCC
    occ_slab = lax.dynamic_slice_in_dim(occ_energy, slab_start, NOCC)
    pair_energy = jnp.repeat(occ_slab, NVIRT) - jnp.tile(virt_energy, NOCC)
    row_energy = lax.dynamic_slice_in_dim(pair_energy, lax.axis_index("blk") * pair_cols, pair_cols)
    col_energy = lax.dynamic_slice_in_dim(pair_energy, sub_index * quarter, quarter)
    return coulomb / (row_energy[:, None] + col_energy[None, :])


def solution(mesh):
    in_specs = (
        P("blk", "sub", None, None),
        P("blk", "sub", None),
        P(None, "sub", None, None),
        P(),
        P(),
        P(),
    )
    out_specs = P("blk", "sub")
    return jax.shard_map(shards, mesh=mesh, in_specs=in_specs, out_specs=out_specs, check_vma=False)
```

profile of v0, /device:TPU:0, one launch (start us, length us, event | category | flops | bytes accessed | tf_op | source)
XLA Modules:
  0.0 1643.7 jit_solution(12217533241742672340)
XLA Ops:
  12.4 10.1 copy.18
  22.5 12.3 reshape.389
  42.1 9.4 copy.23
  51.5 13.8 copy.16
  73.5 23.0 %all-gather.37.cloned.1.call-done = f32[32,128,128]{2,1,0:T(8,128)} async-done(((f32[32,32,128]{2,1,0:T(8,128)}), f32[32,128,128]{2,1,0:T(8,128)}) %all-gather.37.cloned.1.call-update) | async-done | bytes 2097168 | tf_op jit(solution)/shard_map/all_gather | solution.py:55
  99.7 315.9 %custom-call.4 = f32[32,1,128,128]{2,3,1,0:T(8,128)} custom-call(f32[32,1,128,128]{3,2,1,0:T(8,128)} %bitcast_select_fusion), custom_call_target="InvertDiagBlocksLowerTriangular" | custom-call | tf_op jit(solution)/shard_map/jit(_solve_triangular)/vmap()/triangular_solve | solution.py:61
  422.6 11.4 reduce.8
  434.0 13.0 reshape.390
  447.0 7.6 copy.22
  705.5 7.3 fusion.48
  725.3 7.3 fusion.47
  745.1 7.3 fusion.46
  764.8 7.3 fusion.45
  785.7 10.9 fusion.44
  810.1 10.9 fusion.43
  834.8 10.9 fusion.42
  859.1 10.9 fusion.41
  878.1 8.6 fusion.40
  894.9 8.6 fusion.39
  911.8 8.6 fusion.38
  928.5 8.6 fusion.37
  947.1 480.5 %all-gather.35.cloned.1.call-done = f32[1024,6144]{1,0:T(8,128)} async-done(((f32[1024,768]{1,0:T(8,128)}), f32[1024,6144]{1,0:T(8,128)}) %all-gather.35.cloned.1.call-update) | async-done | bytes 25165840 | tf_op jit(solution)/shard_map/all_gather | solution.py:84
  1427.6 66.3 %fusion.77 = f32[768,6144]{1,0:T(8,128)} fusion(f32[1024,768]{1,0:T(8,128)} %bitcast.777, f32[1024,6144]{1,0:T(8,128)} %all-gather.35.cloned.1.call-done), kind=kOutput, calls=%fused_computation.243 | convolution fusion | flops 57982058496 | bytes 47185920 | tf_op jit(solution)/shard_map/dot_general | solution.py:19
  1495.9 135.9 %reduce-scatter.2.cloned.1.call-done = f32[768,1536]{1,0:T(8,128)} async-done(((f32[768,6144]{1,0:T(8,128)}), f32[768,1536]{1,0:T(8,128)}) %reduce-scatter.2.cloned.1.call-update) | async-done | bytes 4718608 | tf_op jit(solution)/shard_map/reduce_scatter | solution.py:85
  (145 shorter events, 422.4 us)
Async XLA Ops:
  6.5 1.9 copy-start
  34.8 387.3 %all-to-all-start = ((f32[8,1,98304]{2,1,0:T(1,128)}), f32[8,1,98304]{2,1,0:T(1,128)S(1)}, u32[]{:S(2)}, u32[]{:S(2)}) async-start(f32[8,1,98304]{2,1,0:T(1,128)} %reshape.389), calls=%async_computation | async-start | bytes 6291456 | tf_op jit(solution)/shard_map/all_to_all | solution.py:46
  42.1 54.5 %all-gather.37.cloned.1.call-start = ((), (), s32[]{:S(2)}) async-start(), calls=%async_computation.4 | async-start | bytes 2621440 | tf_op jit(solution)/shard_map/all_gather | solution.py:55
  72.5 1355.1 %all-gather.35.cloned.1.call-start = ((), (), s32[]{:S(2)}) async-start(), calls=%async_computation.2 | async-start | bytes 28311552 | tf_op jit(solution)/shard_map/all_gather | solution.py:84
  455.6 309.2 %copy-start.2 = (f32[8,4,1,32,768]{4,3,1,0,2:T(8,128)}, f32[8,4,1,32,768]{4,3,1,0,2:T(8,128)S(1)}, u32[]{:S(2)}) copy-start(f32[8,4,1,32,768]{4,3,1,0,2:T(8,128)S(1)} %copy.20) | copy-start | bytes 9437188
  947.1 684.7 %reduce-scatter.2.cloned.1.call-start = ((), (), s32[]{:S(2)}) async-start(), calls=%async_computation.3 | async-start | bytes 23592960 | tf_op jit(solution)/shard_map/reduce_scatter | solution.py:85
  1493.9 1.7 copy-start.3
  1493.9 143.0 %copy-start.1 = (f32[4,1,32,6144]{3,2,1,0:T(8,128)S(1)}, f32[4,1,32,6144]{3,2,1,0:T(8,128)}, u32[]{:S(2)}) copy-start(f32[4,1,32,6144]{3,2,1,0:T(8,128)} %param.6) | copy-start | bytes 9437188
Sparse Core Ops, SparseCore 0:
  72.6 23.9 all-gather.36
  947.2 480.3 all-gather.34
  1494.1 137.6 reduce-scatter.1
where the time goes:
time: 1650 us; the launch traced here: 1640 us
  waiting for transfers between devices  639 us (39%)
  other arithmetic  337 us (20%)
  matrix products  301 us (18%)
  blocking collectives  214 us (13%)
  local copies, waits for them, and re-layouts  130 us (8%)
    all_gather x1, waiting for transfers between devices, shards(): lax.all_gather(own_part, 'blk', axis=1, tiled=True)  480 us
    another operation x3, other arithmetic, shards(): jax.scipy.linalg.solve_triangular(diag_blocks, identity, lower=True)  319 us
    all_gather x32, blocking collectives, advance(): lax.all_gather(updated[None], 'sub', axis=0, tiled=True)  214 us
    dot_general x31, matrix products, advance(): jnp.dot(factor_part, solved[:reach].reshape(width, pair_cols), precision=...  182 us
    reduce_scatter x1, waiting for transfers between devices, shards(): coulomb = lax.psum_scatter(product, 'sub', scatter_dimension=1, tiled=True)  136 us
    dot_general x1, matrix products, transposed_dot(): lax.dot_general(left, right, (((0,), (0,)), ((), ())), precision=PRECISE)  66.3 us
    slice x27, local copies, waits for them, and re-layouts, advance(): solved[:reach].reshape(width, pair_cols)  48.7 us
    dot_general x32, matrix products, advance(): solved_round = jnp.dot(inverse, round_block, precision=PRECISE)  42 us
  transfers between devices with their start and end apart: 4, of which 3 were waited for; matrix products, arithmetic and copies ran while one was open for 22% of the time, Pallas kernels for 0%

commit v1 on v0

--- a/solution.py
+++ b/solution.py
@@ -81,7 +81,7 @@
     own_part = lax.dynamic_index_in_dim(solved_full, sub_index, 1, keepdims=False).reshape(
         rounds * piece_len, pair_cols
     )
-    product = transposed_dot(own_part, lax.all_gather(own_part, "blk", axis=1, tiled=True))
+    product = transposed_dot(own_part, jnp.concatenate(lax.all_gather(own_part, "blk"), axis=1))
     coulomb = lax.psum_scatter(product, "sub", scatter_dimension=1, tiled=True)
     slab_start = slab_index[0] * NOCC
     occ_slab = lax.dynamic_slice_in_dim(occ_energy, slab_start, NOCC)

time: 1650 us -> 1740 us (1.055)
  matrix products: 301 us -> 357 us
  local copies, waits for them, and re-layouts: 130 us -> 155 us
    dot_general x1, matrix products: 66.3 us -> 122 us  [transposed_dot(): lax.dot_general(left, right, (((0,), (0,)), ((), ())), precision=PRECISE)]
    all_gather x0 -> x1, local copies, waits for them, and re-layouts: none -> 24.7 us  [shards(): lax.all_gather(own_part, 'blk')]
    unnamed x11 -> x13, local copies, waits for them, and re-layouts: 36.6 us -> 36.6 us
  transfers between devices with their start and end apart: 4 -> 4, of which waited for: 3 -> 3; matrix products, arithmetic and copies ran while one was open for 22% -> 21% of each run, Pallas kernels for 0% -> 0%
where the time goes in v1:
time: 1740 us; the launch traced here: 1720 us
  waiting for transfers between devices  639 us (37%)
  matrix products  357 us (21%)
  other arithmetic  337 us (19%)
  blocking collectives  214 us (12%)
  local copies, waits for them, and re-layouts  155 us (9%)
    all_gather x1, waiting for transfers between devices, shards(): lax.all_gather(own_part, 'blk')  480 us
    another operation x3, other arithmetic, shards(): jax.scipy.linalg.solve_triangular(diag_blocks, identity, lower=True)  319 us
    all_gather x32, blocking collectives, advance(): lax.all_gather(updated[None], 'sub', axis=0, tiled=True)  214 us
    dot_general x31, matrix products, advance(): jnp.dot(factor_part, solved[:reach].reshape(width, pair_cols), precision=...  182 us
    reduce_scatter x1, waiting for transfers between devices, shards(): coulomb = lax.psum_scatter(product, 'sub', scatter_dimension=1, tiled=True)  136 us
    dot_general x1, matrix products, transposed_dot(): lax.dot_general(left, right, (((0,), (0,)), ((), ())), precision=PRECISE)  122 us
    slice x27, local copies, waits for them, and re-layouts, advance(): solved[:reach].reshape(width, pair_cols)  48.6 us
    dot_general x32, matrix products, advance(): solved_round = jnp.dot(inverse, round_block, precision=PRECISE)  42 us
  transfers between devices with their start and end apart: 4, of which 3 were waited for; matrix products, arithmetic and copies ran while one was open for 21% of the time, Pallas kernels for 0%

profile of v1, /device:TPU:0, one launch (start us, length us, event | category | flops | bytes accessed | tf_op | source)
XLA Modules:
  0.0 1723.9 jit_solution(14020297798425372031)
XLA Ops:
  12.4 10.0 copy.23
  22.4 12.3 reshape.398
  42.1 9.4 copy.31
  51.5 13.7 copy.21
  73.5 23.0 %all-gather.37.cloned.1.call-done = f32[32,128,128]{2,1,0:T(8,128)} async-done(((f32[32,32,128]{2,1,0:T(8,128)}), f32[32,128,128]{2,1,0:T(8,128)}) %all-gather.37.cloned.1.call-update) | async-done | bytes 2097168 | tf_op jit(solution)/shard_map/all_gather | solution.py:55
  99.7 315.9 %custom-call.4 = f32[32,1,128,128]{2,3,1,0:T(8,128)} custom-call(f32[32,1,128,128]{3,2,1,0:T(8,128)} %bitcast_select_fusion), custom_call_target="InvertDiagBlocksLowerTriangular" | custom-call | tf_op jit(solution)/shard_map/jit(_solve_triangular)/vmap()/triangular_solve | solution.py:61
  422.4 11.2 reduce.8
  433.7 13.0 reshape.399
  446.7 7.6 copy.29
  705.2 7.3 fusion.48
  725.0 7.3 fusion.47
  744.8 7.3 fusion.46
  785.4 10.9 fusion.44
  809.8 10.9 fusion.43
  834.4 10.9 fusion.42
  858.8 10.9 fusion.41
  877.8 8.6 fusion.40
  894.5 8.6 fusion.39
  911.5 8.6 fusion.38
  928.2 8.6 fusion.37
  946.8 480.5 %all-gather.35.cloned.1.call-done = f32[8,1024,768]{2,1,0:T(8,128)} async-done(((f32[1,1024,768]{2,1,0:T(8,128)}), f32[8,1024,768]{2,1,0:T(8,128)}) %all-gather.35.cloned.1.call-update) | async-done | bytes 25165840 | tf_op jit(solution)/shard_map/all_gather | solution.py:84
  1427.3 24.7 %copy.27 = f32[8,1024,768]{1,2,0:T(8,128)} copy(f32[8,1024,768]{2,1,0:T(8,128)} %all-gather.35.cloned.1.call-done) | data formatting | bytes 50331648 | tf_op jit(solution)/shard_map/all_gather | solution.py:84
  1452.0 122.0 %fusion.77 = f32[768,6144]{1,0:T(8,128)} fusion(f32[1024,768]{1,0:T(8,128)S(1)} %bitcast.785, f32[1024,6144]{0,1:T(8,128)} %bitcast.743), kind=kOutput, calls=%fused_computation.243 | convolution fusion | flops 57982058496 | bytes 47185920 | tf_op jit(solution)/shard_map/dot_general | solution.py:19
  1576.0 135.9 %reduce-scatter.2.cloned.1.call-done = f32[768,1536]{1,0:T(8,128)} async-done(((f32[768,6144]{1,0:T(8,128)}), f32[768,1536]{1,0:T(8,128)}) %reduce-scatter.2.cloned.1.call-update) | async-done | bytes 4718608 | tf_op jit(solution)/shard_map/reduce_scatter | solution.py:85
  (148 shorter events, 429.6 us)
Async XLA Ops:
  6.5 1.9 copy-start
  34.7 387.2 %all-to-all-start = ((f32[8,1,98304]{2,1,0:T(1,128)}), f32[8,1,98304]{2,1,0:T(1,128)S(1)}, u32[]{:S(2)}, u32[]{:S(2)}) async-start(f32[8,1,98304]{2,1,0:T(1,128)} %reshape.398), calls=%async_computation | async-start | bytes 6291456 | tf_op jit(solution)/shard_map/all_to_all | solution.py:46
  42.0 54.5 %all-gather.37.cloned.1.call-start = ((), (), s32[]{:S(2)}) async-start(), calls=%async_computation.4 | async-start | bytes 2621440 | tf_op jit(solution)/shard_map/all_gather | solution.py:55
  72.4 1354.8 %all-gather.35.cloned.1.call-start = ((), (), s32[]{:S(2)}) async-start(), calls=%async_computation.2 | async-start | bytes 28311552 | tf_op jit(solution)/shard_map/all_gather | solution.py:84
  455.3 309.2 %copy-start.2 = (f32[8,4,1,32,768]{4,3,1,0,2:T(8,128)}, f32[8,4,1,32,768]{4,3,1,0,2:T(8,128)S(1)}, u32[]{:S(2)}) copy-start(f32[8,4,1,32,768]{4,3,1,0,2:T(8,128)S(1)} %copy.25) | copy-start | bytes 9437188
  946.7 505.2 %copy-start.3 = (f32[32,1,32,768]{3,2,1,0:T(8,128)S(1)}, f32[32,1,32,768]{3,2,1,0:T(8,128)}, u32[]{:S(2)}) copy-start(f32[32,1,32,768]{3,2,1,0:T(8,128)} %constant_dynamic-slice_fusion) | copy-start | bytes 9437188
  946.8 765.1 %reduce-scatter.2.cloned.1.call-start = ((), (), s32[]{:S(2)}) async-start(), calls=%async_computation.3 | async-start | bytes 23592960 | tf_op jit(solution)/shard_map/reduce_scatter | solution.py:85
  1574.0 1.7 copy-start.4
  1574.0 143.0 %copy-start.1 = (f32[4,1,32,6144]{3,2,1,0:T(8,128)S(1)}, f32[4,1,32,6144]{3,2,1,0:T(8,128)}, u32[]{:S(2)}) copy-start(f32[4,1,32,6144]{3,2,1,0:T(8,128)} %param.6) | copy-start | bytes 9437188
Sparse Core Ops, SparseCore 0:
  72.6 23.9 all-gather.36
  946.9 480.3 all-gather.34
  1574.1 137.6 reduce-scatter.1
